TPU v7x, 32 devices: a whole 2x2x4 slice. The times are simulated.
32 devices in a mesh: row: 4 (over y, x), col: 8 (over z, core).
Axes of the slice: x: 2, y: 2, z: 4, core: 2. Of those that a mesh axis runs over, the one named last changes fastest.
Arguments:
- adjacency: int32 [8192, 256], P('row', 'col'), may hold values from -2147483648 to 2147483647, as said below
- seed_mask: int32 [8192], P('col'), may hold values 0 or 1
- source: int32 [1], replicated, may hold values from 0 to 8191
Outputs:
- levels: int32 [8192], P('col')
- parents: int32 [8192], P('col')
Inputs may be any that keep to these rules, and one draw needn't show every extreme that they name: adjacency is symmetric (edge(u, v) = edge(v, u)); it is the union of 131072 Kronecker edges whose endpoints pick one of four quadrants per bit with weights 57, 19, 19, 5 out of 100, vertex labels not permuted, so low ids carry most edges; each word is a 32-bit pattern read as a signed int32.
All inputs are finite; a program needn't handle non-finite values.
Results may differ from a plain program's by a relative error of at most 0.000001.
Values may be sent and summed in bfloat16 or wider, within the bound.
A program may use at most 64 MiB of HBM per device.

v0:
```python
import math

import jax
import jax.numpy as jnp
from jax import lax
from jax.sharding import PartitionSpec as P

LEVELS = 4


absent = 1073741824


def from_root(block, axis, source):
    block = jnp.where(lax.axis_index(axis) == source, block, jnp.zeros_like(block))
    return lax.psum(block, axis)


def unpack(words):
    shifts = jnp.arange(32, dtype=jnp.int32)
    bit_table = jnp.bitwise_and(jnp.right_shift(words[..., None], shifts), 1)
    return bit_table.reshape(words.shape[:-1] + (words.shape[-1] * 32,))


def nearest_sources(adjacency, active, first_row):
    height = adjacency.shape[0]
    width = adjacency.shape[1] * 32
    block_rows = math.gcd(height, 256)

    def sweep_block(lowest, block_id):
        offset = block_id * block_rows
        tile_words = lax.dynamic_slice_in_dim(adjacency, offset, block_rows, 0)
        marks = lax.dynamic_slice_in_dim(active, offset, block_rows, 0)

        def scan_tile(current):
            row_ids = first_row + offset + jnp.arange(block_rows, dtype=jnp.int32)
            linked = unpack(tile_words) * marks[:, None] > 0
            found = jnp.min(jnp.where(linked, row_ids[:, None], absent), axis=0)
            return jnp.minimum(current, found)

        def keep_tile(current):
            return current

        lowest = lax.cond(jnp.any(marks > 0), scan_tile, keep_tile, lowest)
        return (lowest, None)

    start_value = jnp.full((width,), absent, jnp.int32)
    lowest, unused = lax.scan(
        sweep_block, start_value, jnp.arange(height // block_rows, dtype=jnp.int32)
    )
    return lowest


def row_frontier_of(frontier):
    col_count = lax.axis_size("col")
    row_count = lax.axis_size("row")
    owner_count = col_count // row_count
    blocks = []
    for part_no in range(owner_count):
        root_col = lax.axis_index("row") * owner_count + part_no
        blocks.append(from_root(frontier, "col", root_col))
    row_payload = jnp.concatenate(blocks, axis=0)
    return row_payload


def local(adjacency, seed_mask, source):
    height = adjacency.shape[0]
    width = adjacency.shape[1] * 32
    first_row = (lax.axis_index("row") * height).astype(jnp.int32)
    first_col = (lax.axis_index("col") * width).astype(jnp.int32)
    vertex_ids = first_col + jnp.arange(width, dtype=jnp.int32)
    reached = (seed_mask > 0) | (vertex_ids == source[0])
    levels = jnp.where(reached, 0, -1).astype(jnp.int32)
    parents = jnp.where(reached, vertex_ids, -1).astype(jnp.int32)
    frontier = reached.astype(jnp.int32)
    for depth_no in range(1, LEVELS + 1):
        row_frontier = row_frontier_of(frontier)
        nearest = nearest_sources(adjacency, row_frontier, first_row)
        nearest = lax.pmin(nearest, "row")
        fresh = (nearest < absent) & (levels < 0)
        levels = jnp.where(fresh, depth_no, levels).astype(jnp.int32)
        parents = jnp.where(fresh, nearest, parents).astype(jnp.int32)
        frontier = fresh.astype(jnp.int32)
    return (levels, parents)


def solution(mesh):
    in_specs = (P("row", "col"), P("col"), P())
    out_specs = (P("col"), P("col"))
    return jax.shard_map(local, mesh=mesh, in_specs=in_specs, out_specs=out_specs, check_vma=False)
```

profile of v0, /device:TPU:0, one launch (start us, length us, event | category | flops | bytes accessed | tf_op | source)
XLA Modules:
  0.0 188.6 jit_solution(4440167789065246323)
XLA Ops:
  1.4 10.8 %all-reduce.3 = (s32[1024]{0:T(1024)S(1)}, s32[1024]{0:T(1024)S(1)}) all-reduce(s32[1024]{0:T(1024)S(1)} %convert_select_fusion.6, s32[1024]{0:T(1024)S(1)} %get-tuple-element.372), channel_id=1, replica_groups=mesh['row'=4,'col'=8] {'col'}, use_global_device_ids=true, to_apply=%region_1.2 | all-reduce | flops 2048 | bytes 16384 | tf_op jit(solution)/shard_map/psum | solution.py:16
  12.2 27.9 %while.52 = (s32[]{:T(128)}, s32[1024]{0:T(1024)S(1)}, s32[8]{0:T(128)S(1)}, s32[2048]{0:T(1024)S(1)}, s32[2048,32]{0,1:T(8,128)}, /*index=5*/s32[]{:T(128)}, s32[]{:T(128)}, s32[1]{0:T(128)}, s32[]{:T(128)}, s32[]{:T(128)}) while((s32[]{:T(128)}, s32[1024]{0:T(1024)S(1)}, s32[8]{0:T(128)S(1)}, s32[2048]{0:T(1024)S(1)}, s32[2048,32]{0,1:T(8,128)}, ...), condition=%wide.region_7.8_spmd, body=%wide.region_2.7_spmd.sunk | while | flops 1573639 | bytes 128245 | solution.py:48
  23.0 1.6 conditional.8
  23.0 0.9 constant_dynamic-slice_fusion
  27.3 1.6 conditional.8
  27.3 0.9 constant_dynamic-slice_fusion
  34.3 1.6 conditional.8
  34.3 0.9 constant_dynamic-slice_fusion
  38.5 1.6 conditional.8
  38.6 0.8 constant_dynamic-slice_fusion
  40.1 5.6 %pmin.28 = s32[1024]{0:T(1024)S(1)} all-reduce(s32[1024]{0:T(1024)S(1)} %get-tuple-element.274), channel_id=1, replica_groups=mesh['row'=4,'col'=8] {'row'}, use_global_device_ids=true, to_apply=%region_8.9 | all-reduce | flops 1024 | bytes 8192 | tf_op jit(solution)/shard_map/pmin | solution.py:79
  45.7 6.3 %all-reduce.2 = (s32[1024]{0:T(1024)S(1)}, s32[1024]{0:T(1024)S(1)}) all-reduce(s32[1024]{0:T(1024)S(1)} %convert_select_fusion.4, s32[1024]{0:T(1024)S(1)} %get-tuple-element.370), channel_id=1, replica_groups=mesh['row'=4,'col'=8] {'col'}, use_global_device_ids=true, to_apply=%region_10.11 | all-reduce | flops 2048 | bytes 16384 | tf_op jit(solution)/shard_map/psum | solution.py:16
  52.1 32.7 %while.53 = (s32[]{:T(128)}, s32[1024]{0:T(1024)S(1)}, s32[8]{0:T(128)S(1)}, s32[2048]{0:T(1024)S(1)}, s32[2048,32]{0,1:T(8,128)}, /*index=5*/s32[]{:T(128)}, s32[]{:T(128)}, s32[1]{0:T(128)}, s32[]{:T(128)}, s32[]{:T(128)}) while((s32[]{:T(128)}, s32[1024]{0:T(1024)S(1)}, s32[8]{0:T(128)S(1)}, s32[2048]{0:T(1024)S(1)}, ...), condition=%wide.region_16.17_spmd, body=%wide.region_11.16_spmd.sunk | while | flops 1573639 | bytes 128245 | solution.py:48
  54.8 1.6 conditional.9
  54.8 0.9 constant_dynamic-slice_fusion.1
  59.1 1.6 conditional.9
  59.1 0.9 constant_dynamic-slice_fusion.1
  63.4 1.6 conditional.9
  63.4 0.9 constant_dynamic-slice_fusion.1
  67.6 1.6 conditional.9
  67.7 0.9 constant_dynamic-slice_fusion.1
  71.9 1.6 conditional.9
  71.9 0.9 constant_dynamic-slice_fusion.1
  76.2 1.6 conditional.9
  76.2 0.9 constant_dynamic-slice_fusion.1
  80.5 1.6 conditional.9
  80.5 0.9 constant_dynamic-slice_fusion.1
  84.8 5.6 %pmin.29 = s32[1024]{0:T(1024)S(1)} all-reduce(s32[1024]{0:T(1024)S(1)} %get-tuple-element.275), channel_id=1, replica_groups=mesh['row'=4,'col'=8] {'row'}, use_global_device_ids=true, to_apply=%region_17.18 | all-reduce | flops 1024 | bytes 8192 | tf_op jit(solution)/shard_map/pmin | solution.py:79
  90.4 8.9 %all-reduce.1 = (s32[1024]{0:T(1024)S(1)}, s32[1024]{0:T(1024)S(1)}) all-reduce(s32[1024]{0:T(1024)S(1)} %convert_select_fusion.2, s32[1024]{0:T(1024)S(1)} %get-tuple-element.368), channel_id=1, replica_groups=mesh['row'=4,'col'=8] {'col'}, use_global_device_ids=true, to_apply=%region_19.20 | all-reduce | flops 2048 | bytes 16384 | tf_op jit(solution)/shard_map/psum | solution.py:16
  99.4 34.2 %while.54 = (s32[]{:T(128)}, s32[1024]{0:T(1024)S(1)}, s32[8]{0:T(128)S(1)}, s32[2048]{0:T(1024)S(1)}, s32[2048,32]{0,1:T(8,128)}, /*index=5*/s32[]{:T(128)}, s32[]{:T(128)}, s32[1]{0:T(128)}, s32[]{:T(128)}, s32[]{:T(128)}) while((s32[]{:T(128)}, s32[1024]{0:T(1024)S(1)}, s32[8]{0:T(128)S(1)}, s32[2048]{0:T(1024)S(1)}, ...), condition=%wide.region_25.26_spmd, body=%wide.region_20.25_spmd.sunk | while | flops 1573639 | bytes 128245 | solution.py:48
  102.0 1.6 conditional.10
  102.1 0.9 constant_dynamic-slice_fusion.2
  106.3 1.6 conditional.10
  106.3 0.9 constant_dynamic-slice_fusion.2
  110.6 1.6 conditional.10
  110.6 0.9 constant_dynamic-slice_fusion.2
  114.9 1.6 conditional.10
  114.9 0.9 constant_dynamic-slice_fusion.2
  119.2 1.6 conditional.10
  119.2 0.9 constant_dynamic-slice_fusion.2
  123.5 1.6 conditional.10
  123.5 0.9 constant_dynamic-slice_fusion.2
  127.7 1.6 conditional.10
  127.8 0.9 constant_dynamic-slice_fusion.2
  132.0 1.6 conditional.10
  133.6 8.2 %pmin.30 = s32[1024]{0:T(1024)S(1)} all-reduce(s32[1024]{0:T(1024)S(1)} %get-tuple-element.276), channel_id=1, replica_groups=mesh['row'=4,'col'=8] {'row'}, use_global_device_ids=true, to_apply=%region_26.27 | all-reduce | flops 1024 | bytes 8192 | tf_op jit(solution)/shard_map/pmin | solution.py:79
  141.8 6.4 %all-reduce = (s32[1024]{0:T(1024)S(1)}, s32[1024]{0:T(1024)S(1)}) all-reduce(s32[1024]{0:T(1024)S(1)} %convert_select_fusion, s32[1024]{0:T(1024)S(1)} %get-tuple-element.366), channel_id=1, replica_groups=mesh['row'=4,'col'=8] {'col'}, use_global_device_ids=true, to_apply=%region_28.29 | all-reduce | flops 2048 | bytes 16384 | tf_op jit(solution)/shard_map/psum | solution.py:16
  148.2 34.2 %while.55 = (s32[]{:T(128)}, s32[1024]{0:T(1024)S(1)}, s32[8]{0:T(128)S(1)}, s32[2048]{0:T(1024)S(1)}, s32[2048,32]{0,1:T(8,128)}, /*index=5*/s32[]{:T(128)}, s32[]{:T(128)}, s32[1]{0:T(128)}, s32[]{:T(128)}, s32[]{:T(128)}) while((s32[]{:T(128)}, s32[1024]{0:T(1024)S(1)}, s32[8]{0:T(128)S(1)}, s32[2048]{0:T(1024)S(1)}, ...), condition=%wide.region_34.35_spmd, body=%wide.region_29.34_spmd.sunk | while | flops 1573639 | bytes 128245 | solution.py:48
  150.9 1.6 conditional.11
  150.9 0.9 constant_dynamic-slice_fusion.3
  155.1 1.6 conditional.11
  155.2 0.9 constant_dynamic-slice_fusion.3
  159.4 1.6 conditional.11
  159.4 0.9 constant_dynamic-slice_fusion.3
  163.7 1.6 conditional.11
  163.7 0.9 constant_dynamic-slice_fusion.3
  168.0 1.6 conditional.11
  168.0 0.9 constant_dynamic-slice_fusion.3
  172.3 1.6 conditional.11
  172.3 0.9 constant_dynamic-slice_fusion.3
  176.6 1.6 conditional.11
  176.6 0.9 constant_dynamic-slice_fusion.3
  180.8 1.6 conditional.11
  182.4 5.6 %pmin.31 = s32[1024]{0:T(1024)S(1)} all-reduce(s32[1024]{0:T(1024)S(1)} %get-tuple-element.277), channel_id=1, replica_groups=mesh['row'=4,'col'=8] {'row'}, use_global_device_ids=true, to_apply=%region_35.36 | all-reduce | flops 1024 | bytes 8192 | tf_op jit(solution)/shard_map/pmin | solution.py:79
  (202 shorter events, 65.8 us)
Async XLA Ops:
  0.6 0.7 copy-start
where the time goes:
time: 191 us; the launch traced here: 189 us
  blocking collectives  57.4 us (30%)
  local copies, waits for them, and re-layouts  46.4 us (24%)
  loops' own time  42 us (22%)
  other arithmetic  41.4 us (22%)
    another operation x4, loops' own time, nearest_sources(): lax.scan(sweep_block, start_value, jnp.arange(height // block_rows, dtype...  41.3 us
    psum x4, blocking collectives, from_root(): return lax.psum(block, axis)  32.5 us
    pmin x4, blocking collectives, local(): nearest = lax.pmin(nearest, 'row')  25 us
    dynamic_slice x27, local copies, waits for them, and re-layouts, sweep_block(): tile_words = lax.dynamic_slice_in_dim(adjacency, offset, block_rows, 0)  23.7 us
    reduce_or x32, other arithmetic, sweep_block(): lowest = lax.cond(jnp.any(marks > 0), scan_tile, keep_tile, lowest)  23.5 us
    dynamic_slice x32, local copies, waits for them, and re-layouts, nearest_sources(): lax.scan(sweep_block, start_value, jnp.arange(height // block_rows, dtype...  20.7 us
    reduce_min x27, other arithmetic, scan_tile(): found = jnp.min(jnp.where(linked, row_ids[:, None], absent), axis=0)  16.9 us

commit v1 on v0

v1 whole, which is shorter than its diff:
```python
import functools

import jax
import jax.numpy as jnp
from jax import lax
from jax.experimental import pallas as pl
from jax.experimental.pallas import tpu as pltpu
from jax.sharding import PartitionSpec as P

LEVELS = 4
MESH = pl.DeviceIdType.MESH
PAIR = 0x10001


def log2(n):
    return n.bit_length() - 1


def gather_lanes(x, idx):
    return jnp.take_along_axis(x, idx, axis=1)


def repeat(n, body, init):
    if n <= 4:
        for i in range(n):
            init = body(i, init)
        return init
    return lax.fori_loop(0, n, body, init)


def merge(low, high):
    rest = ~low[0]
    out = [low[0] | high[0]]
    for a, b in zip(low[1:], high[1:]):
        out.append(a | (b & rest))
    out.append(high[0] & rest)
    return out


def kernel(R, C, adj_ref, seed_ref, src_ref, lev_ref, par_ref,
           words_ref, col_buf, row_buf, key_buf,
           col_send, col_recv, row_send, row_recv, key_send, key_recv):
    me_r = lax.axis_index("row")
    me_c = lax.axis_index("col")
    height, wd = adj_ref.shape
    G = 128 // wd
    K = height // 256
    KG = K // G
    NB = 128 // K
    NTC = 16 // NB
    NTR = 4 // G
    total = R * height

    barrier = pltpu.get_barrier_semaphore()
    for step in range(1, C):
        pl.semaphore_signal(barrier, inc=1, device_id={"col": lax.rem(me_c + step, C)}, device_id_type=MESH)
    for step in range(1, R):
        pl.semaphore_signal(barrier, inc=1, device_id={"row": lax.rem(me_r + step, R)}, device_id_type=MESH)

    lane = lax.broadcasted_iota(jnp.int32, (8, 128), 1)
    sub = lax.broadcasted_iota(jnp.int32, (8, 128), 0)
    zero = jnp.zeros((8, 128), jnp.int32)

    leaves = height // 8 // G

    def compact(i, carry):
        for t in range(8):
            j = i * 8 + t
            parts = [adj_ref[pl.ds(g * leaves + j, 8, stride=height // 8), :] for g in range(G)]
            words_ref[j] = parts[0] if G == 1 else jnp.concatenate(parts, axis=1)
        return carry

    lax.fori_loop(0, leaves // 8, compact, 0)

    source = src_ref[0]
    first = me_c * (wd * 32)
    word_of = lane % wd
    words = zero
    for q in range(seed_ref.shape[0] // 8):
        vid = first + (sub + 8 * q) * 128 + lane
        x = jnp.where((seed_ref[pl.ds(8 * q, 8), :] > 0) | (vid == source), 1, 0)
        x = x << (lane % 32)
        for sh in (1, 2, 4, 8, 16):
            x = x | pltpu.roll(x, 128 - sh, 1)
        x = gather_lanes(x, 32 * (word_of % 4))
        words = words | jnp.where(word_of // 4 == sub + 8 * q, x, 0)
    for sh in (4, 2, 1):
        words = words | pltpu.roll(words, sh, 0)

    def spread_col(words):
        def step(k, acc_all):
            acc = zero
            for b in range(32):
                bit = (1 << b) if b < 31 else -(1 << 31)
                acc = acc | jnp.where((words_ref[k * 32 + b] & words) != 0, bit, 0)
            sh = 1
            while sh < wd:
                acc = acc | pltpu.roll(acc, 128 - sh, 1)
                sh *= 2
            got = gather_lanes(acc, wd * ((lane % K) // KG))
            return acc_all | jnp.where(lane % KG == k, got, 0)

        nxt = repeat(KG, step, zero)
        at = me_r * (height // 32) + sub * K + lane % K - me_c * wd
        now = gather_lanes(words, jnp.clip(at, 0, wd - 1))
        now = jnp.where((at >= 0) & (at < wd), now, 0)
        nxt = nxt | now
        tiles = []
        for t in range(NTC):
            sh = t * NB + lane // K
            tiles.append((lax.shift_right_logical(nxt, sh) & PAIR)
                         | ((lax.shift_right_logical(now, sh) & PAIR) << 1))
        return tiles

    def exchange(axis, count, me, slot, send, recv):
        copies = []
        order = sorted(range(1, count), key=lambda s: -min(s, count - s))
        for step in order:
            copy = pltpu.make_async_remote_copy(
                src_ref=slot.at[0], dst_ref=slot.at[step],
                send_sem=send.at[step], recv_sem=recv.at[step],
                device_id={axis: lax.rem(me + step, count)}, device_id_type=MESH)
            copy.start()
            copies.append(copy)
        return copies

    def join_col(slot, copies):
        for copy in copies:
            copy.wait_recv()
        nxt = zero
        now = zero
        for t in range(NTC):
            code = slot[0, t]
            for step in range(1, C):
                code = code | slot[step, t]
            sh = t * NB + lane // K
            nxt = nxt | ((code & PAIR) << sh)
            now = now | ((lax.shift_right_logical(code, 1) & PAIR) << sh)
        sh = K
        while sh < 128:
            nxt = nxt | pltpu.roll(nxt, sh, 1)
            now = now | pltpu.roll(now, sh, 1)
            sh *= 2
        return nxt, now

    def row_words(rows, k):
        return gather_lanes(rows, (lane // wd) * KG + k)

    def all_or(x):
        sh = wd
        while sh < 128:
            x = x | pltpu.roll(x, sh, 1)
            sh *= 2
        for sh in (4, 2, 1):
            x = x | pltpu.roll(x, sh, 0)
        return x

    def push(rows):
        def step(k, out):
            f = row_words(rows, k)
            for b in range(32):
                out = out | (words_ref[k * 32 + b] & ((f << (31 - b)) >> 31))
            return out

        out = repeat(KG, step, zero)
        at = me_c * wd + word_of - me_r * (height // 32)
        ok = (at >= 0) & (at < height // 32)
        at = jnp.clip(at, 0, height // 32 - 1)
        own = gather_lanes(rows, at % K)
        return all_or(out | jnp.where(ok & (at // K == sub), own, 0))

    def tournament(rows):
        kbits = log2(KG)

        def step(k, carry):
            f = row_words(rows, k)
            nodes = [[words_ref[k * 32 + b] & ((f << (31 - b)) >> 31)] for b in range(32)]
            while len(nodes) > 1:
                nodes = [merge(nodes[i], nodes[i + 1]) for i in range(0, len(nodes), 2)]
            node = nodes[0]
            fresh = node[0] & ~carry[0]
            rest = ~carry[0]
            out = [carry[0] | node[0]]
            for p in range(5):
                out.append(carry[1 + p] | (node[1 + p] & rest))
            for p in range(kbits):
                out.append(carry[6 + p] | (fresh & -((k >> p) & 1)))
            return tuple(out)

        return list(repeat(KG, step, (zero,) * (6 + kbits)))

    slot_bit = sub * G + lane // wd

    for t, tile in enumerate(spread_col(words)):
        col_buf[0, 0, t] = tile
    pl.semaphore_wait(barrier, R + C - 2)
    pend1 = exchange("col", C, me_c, col_buf.at[0], col_send.at[0], col_recv.at[0])
    s1, s0 = join_col(col_buf.at[0], pend1)

    out = push(s1)
    for t in range(NTR):
        row_buf[0, t] = lax.shift_right_logical(out, slot_bit + t * 8 * G) & 1
    pend2 = exchange("row", R, me_r, row_buf, row_send, row_recv)
    first_two = [tournament(s0), tournament(s1)]
    for copy in pend2:
        copy.wait_recv()
    words = zero
    for t in range(NTR):
        value = row_buf[0, t]
        for step in range(1, R):
            value = value | row_buf[step, t]
        words = words | (value << (slot_bit + t * 8 * G))
    words = all_or(words)

    for t, tile in enumerate(spread_col(words)):
        col_buf[1, 0, t] = tile
    pend3 = exchange("col", C, me_c, col_buf.at[1], col_send.at[1], col_recv.at[1])
    s3, s2 = join_col(col_buf.at[1], pend3)

    nodes = first_two + [tournament(s2), tournament(s3)]
    have = [node[0] for node in nodes]
    planes = list(nodes[0][1:])
    for d in range(1, LEVELS):
        fresh = have[d] & ~have[d - 1]
        planes = [p | (q & fresh) for p, q in zip(planes, nodes[d][1:])]

    def fold(have, planes, sh, axis, size):
        have_hi = [pltpu.roll(x, size - sh, axis) for x in have]
        planes_hi = [pltpu.roll(x, size - sh, axis) for x in planes]
        better = have_hi[0] & ~have[0]
        for a, b in zip(have[1:], have_hi[1:]):
            better = better | (b & ~a)
        keep = ~better
        planes = [(a & keep) | (b & better) for a, b in zip(planes, planes_hi)] + [better]
        return [a | b for a, b in zip(have, have_hi)], planes

    for i in range(log2(G)):
        have, planes = fold(have, planes, wd << i, 1, 128)
    for i in range(3):
        have, planes = fold(have, planes, 1 << i, 0, 8)

    have = [jnp.broadcast_to(x[0:1, :], (8, 128)) for x in have]
    planes = [jnp.broadcast_to(x[0:1, :], (8, 128)) for x in planes]
    for q in range(seed_ref.shape[0] // 8):
        idx = (sub + 8 * q) * 4 + lane // 32

        def bits(x):
            return lax.shift_right_logical(gather_lanes(x, idx), lane % 32) & 1

        key = jnp.full((8, 128), LEVELS * total, jnp.int32)
        for x in have:
            key = key - bits(x) * total
        parent = jnp.full((8, 128), me_r * height, jnp.int32)
        for p, x in enumerate(planes):
            parent = parent + (bits(x) << p)
        key_buf[0, q] = key + parent
    pend4 = exchange("row", R, me_r, key_buf, key_send, key_recv)
    for copy in pend4:
        copy.wait_recv()
    for q in range(seed_ref.shape[0] // 8):
        key = key_buf[0, q]
        for step in range(1, R):
            key = jnp.minimum(key, key_buf[step, q])
        level = jnp.full((8, 128), 1, jnp.int32)
        parent = key
        for d in range(1, LEVELS):
            past = key >= d * total
            level = level + jnp.where(past, 1, 0)
            parent = parent - jnp.where(past, total, 0)
        none = key >= LEVELS * total
        level = jnp.where(none, -1, level)
        parent = jnp.where(none, -1, parent)
        vid = first + (sub + 8 * q) * 128 + lane
        seed = (seed_ref[pl.ds(8 * q, 8), :] > 0) | (vid == source)
        lev_ref[pl.ds(8 * q, 8), :] = jnp.where(seed, 0, level)
        par_ref[pl.ds(8 * q, 8), :] = jnp.where(seed, vid, parent)
    for copy in pend1 + pend2 + pend3 + pend4:
        copy.wait_send()


def solution(mesh):
    R, C = mesh.shape["row"], mesh.shape["col"]

    def local(adjacency, seed_mask, source):
        height, wd = adjacency.shape
        width = seed_mask.shape[0]
        K = height // 256
        G = 128 // wd
        NTC = 16 // (128 // K)
        NTR = 4 // G
        NK = width // 1024
        out = jax.ShapeDtypeStruct((width // 128, 128), jnp.int32)
        vmem = pl.BlockSpec(memory_space=pltpu.VMEM)
        DMA = pltpu.SemaphoreType.DMA
        levels, parents = pl.pallas_call(
            functools.partial(kernel, R, C),
            out_shape=(out, out),
            in_specs=[vmem, vmem, pl.BlockSpec(memory_space=pltpu.SMEM)],
            out_specs=(vmem, vmem),
            scratch_shapes=[
                pltpu.VMEM((height // 8 // G, 8, 128), jnp.int32),
                pltpu.VMEM((2, C, NTC, 8, 128), jnp.int32),
                pltpu.VMEM((R, NTR, 8, 128), jnp.int32),
                pltpu.VMEM((R, NK, 8, 128), jnp.int32),
                DMA((2, C)), DMA((2, C)), DMA((R,)), DMA((R,)), DMA((R,)), DMA((R,)),
            ],
            compiler_params=pltpu.CompilerParams(collective_id=0, has_side_effects=True),
        )(adjacency, seed_mask.reshape(width // 128, 128), source)
        return levels.reshape(width), parents.reshape(width)

    in_specs = (P("row", "col"), P("col"), P())
    out_specs = (P("col"), P("col"))
    return jax.shard_map(local, mesh=mesh, in_specs=in_specs, out_specs=out_specs, check_vma=False)
```

time: 191 us -> 28.6 us (0.15); the launches traced: 189 us -> 28.4 us
  blocking collectives: 57.4 us -> 0 us
  local copies, waits for them, and re-layouts: 46.4 us -> 4.2 us
  loops' own time: 42 us -> 0 us
  other arithmetic: 41.4 us -> 0 us
  Pallas kernels: 0 us -> 22.9 us
    dynamic_slice x59 -> x0, local copies, waits for them, and re-layouts: 44.4 us -> none  [the longest x27 23.7 us: sweep_block(): tile_words = lax.dynamic_slice_in_dim(adjacency, offset, block_rows, 0)]
    another operation x36 -> x0, loops' own time: 42 us -> none  [the longest x4 41.3 us: nearest_sources(): lax.scan(sweep_block, start_value, jnp.arange(height // block_rows, dtype...]
    psum x4 -> x0, blocking collectives: 32.5 us -> none  [from_root(): return lax.psum(block, axis)]
    pmin x4 -> x0, blocking collectives: 25 us -> none  [local(): nearest = lax.pmin(nearest, 'row')]
    reduce_or x32 -> x0, other arithmetic: 23.5 us -> none  [sweep_block(): lowest = lax.cond(jnp.any(marks > 0), scan_tile, keep_tile, lowest)]
    pallas_call x0 -> x1, Pallas kernels: none -> 22.9 us  [local(): pl.pallas_call(functools.partial(kernel, R, C), out_shape=(out, out), in_...]
    reduce_min x27 -> x0, other arithmetic: 16.9 us -> none  [scan_tile(): found = jnp.min(jnp.where(linked, row_ids[:, None], absent), axis=0)]
    unnamed x2 -> x7, local copies, waits for them, and re-layouts: 0.02 us -> 4.2 us
where the time goes in v1:
time: 28.6 us; the launch traced here: 28.4 us
  Pallas kernels  22.9 us (80%)
  local copies, waits for them, and re-layouts  4.2 us (15%)
  between operations  1.29 us (5%)
    pallas_call x1, Pallas kernels, local(): pl.pallas_call(functools.partial(kernel, R, C), out_shape=(out, out), in_...  22.9 us
    unnamed x7, local copies, waits for them, and re-layouts  4.2 us

profile of v1, /device:TPU:0, one launch (start us, length us, event | category | flops | bytes accessed | tf_op | source)
XLA Modules:
  0.0 28.4 jit_solution(8516973398890566102)
XLA Ops:
  1.3 2.3 %copy.5.adj_ref = s32[2048,32]{1,0:T(8,128)} copy(s32[2048,32]{0,1:T(8,128)} %param.3) | data formatting | bytes 524288 | tf_op args[0]
  3.5 22.9 %shard_map.50 = (s32[8,128]{1,0:T(8,128)}, s32[8,128]{1,0:T(8,128)}) custom-call(s32[2048,32]{1,0:T(8,128)} %copy.5.adj_ref, s32[8,128]{1,0:T(8,128)} %bitcast.3, s32[1]{0:T(128)S(6)} %copy.8.src_ref), custom_call_target="tpu_custom_call" | custom-call | tf_op jit(solution)/shard_map/pallas_call | solution.py:295
  26.4 0.0 copy-start.1
  26.4 0.7 %copy-done.1 = s32[8,128]{1,0:T(8,128)S(1)} copy-done((s32[8,128]{1,0:T(8,128)S(1)}, s32[8,128]{1,0:T(8,128)}, u32[]{:S(2)}) %copy-start.1) | copy-done | bytes 4120
  27.1 0.0 copy-start
  27.1 0.6 %copy.9 = s32[1024]{0:T(1024)} copy(s32[1024]{0:T(1024)S(1)} %bitcast.5) | data formatting | bytes 8192
  27.7 0.1 copy-done
  27.8 0.6 %copy.10 = s32[1024]{0:T(1024)} copy(s32[1024]{0:T(1024)S(1)} %bitcast.4) | data formatting | bytes 8192
Async XLA Ops:
  26.4 0.7 %copy-start.1 = (s32[8,128]{1,0:T(8,128)S(1)}, s32[8,128]{1,0:T(8,128)}, u32[]{:S(2)}) copy-start(s32[8,128]{1,0:T(8,128)} %get-tuple-element.4) | copy-start | bytes 12292
  27.1 0.7 %copy-start = (s32[8,128]{1,0:T(8,128)S(1)}, s32[8,128]{1,0:T(8,128)}, u32[]{:S(2)}) copy-start(s32[8,128]{1,0:T(8,128)} %get-tuple-element.5) | copy-start | bytes 12292

commit v2 on v1

v2 whole, which is shorter than its diff:
```python
import functools

import jax
import jax.numpy as jnp
from jax import lax
from jax.experimental import pallas as pl
from jax.experimental.pallas import tpu as pltpu
from jax.sharding import PartitionSpec as P

LEVELS = 4
MESH = pl.DeviceIdType.MESH
PAIR = 0x10001


def log2(n):
    return n.bit_length() - 1


def gather_lanes(x, idx):
    return jnp.take_along_axis(x, idx, axis=1)


def any_of(values):
    values = list(values)
    while len(values) > 1:
        pairs = [values[i] | values[i + 1] for i in range(0, len(values) - 1, 2)]
        values = pairs + values[len(pairs) * 2:]
    return values[0]


def repeat(n, body, init):
    if n <= 4:
        for i in range(n):
            init = body(i, init)
        return init
    return lax.fori_loop(0, n, body, init)


def merge(low, high):
    rest = ~low[0]
    out = [low[0] | high[0]]
    for a, b in zip(low[1:], high[1:]):
        out.append(a | (b & rest))
    out.append(high[0] & rest)
    return out


def kernel(R, C, hbm_ref, seed_ref, src_ref, key_ref,
           adj_ref, load_sem, turn_ref, words_ref, col_buf, row_buf, key_buf,
           col_send, col_recv, row_send, row_recv, key_send, key_recv):
    me_r = lax.axis_index("row")
    me_c = lax.axis_index("col")
    wd, height = hbm_ref.shape
    loads = [pltpu.make_async_copy(hbm_ref.at[:, pl.ds(128 * t, 128)], adj_ref.at[pl.ds(wd * t, wd), :], load_sem.at[t])
             for t in range(height // 128)]
    for load in loads:
        load.start()
    G = 128 // wd
    NI = wd // 32
    NR = height // 1024
    NK = height // 128 // G
    owners = NR // NI
    total = R * height

    barrier = pltpu.get_barrier_semaphore()
    for step in range(1, C):
        pl.semaphore_signal(barrier, inc=1, device_id={"col": lax.rem(me_c + step, C)}, device_id_type=MESH)
    for step in range(1, R):
        pl.semaphore_signal(barrier, inc=1, device_id={"row": lax.rem(me_r + step, R)}, device_id_type=MESH)

    lane = lax.broadcasted_iota(jnp.int32, (8, 128), 1)
    sub = lax.broadcasted_iota(jnp.int32, (8, 128), 0)
    bit = lane % 32
    zero = jnp.zeros((8, 128), jnp.int32)
    source = src_ref[0]
    first = me_c * (wd * 32)

    def seeds(q):
        vid = first + (sub + 8 * q) * 128 + lane
        return (seed_ref[pl.ds(8 * q, 8), :] > 0) | (vid == source), vid

    def block(a, q, t):
        return adj_ref[pl.ds(wd * t + 32 * a + q, 8, stride=4), :]

    def pull(col_set):
        words = []
        for tile in col_set:
            x = tile << bit
            for sh in (1, 2, 4, 8, 16):
                x = x | pltpu.roll(x, 128 - sh, 1)
            words.append([gather_lanes(x, zero + 32 * q) for q in range(4)])
        codes = []
        for h in range(NR):
            accs = [any_of(block(a, q, 8 * h + t) & words[a][q] for a in range(NI) for q in range(4))
                    for t in range(8)]
            for sh in (4, 2, 1):
                low = (sub // sh) % 2 == 0
                half = []
                for t in range(sh):
                    keep = jnp.where(low, accs[t], accs[t + sh])
                    give = jnp.where(low, accs[t + sh], accs[t])
                    if sh == 4:
                        other = pltpu.roll(give, 4, 0)
                    else:
                        other = jnp.where(low, pltpu.roll(give, 8 - sh, 0), pltpu.roll(give, sh, 0))
                    half.append(keep | other)
                accs = half
            code = jnp.where(accs[0] != 0, 1, 0)
            own = me_c == me_r * owners + h // NI
            codes.append(code | jnp.where(own, 3 * col_set[h % NI], 0))
        return [codes[h] | (codes[h + NR // 2] << 16) for h in range(NR // 2)]

    def push(row_set):
        out = [[zero] * 4 for _ in range(NI)]
        for t in range(8 * NR):
            mask = jnp.broadcast_to(row_set[t // 8][t % 8:t % 8 + 1, :], (8, 128))
            for a in range(NI):
                for q in range(4):
                    out[a][q] = out[a][q] | (block(a, q, t) & mask)
        result = []
        for a in range(NI):
            parts = out[a]
            for sh in (64, 32):
                low = (lane // sh) % 2 == 0
                half = []
                for q in range(sh // 32):
                    keep = jnp.where(low, parts[q], parts[q + sh // 32])
                    give = jnp.where(low, parts[q + sh // 32], parts[q])
                    half.append(keep | gather_lanes(give, lane ^ sh))
                parts = half
            x = parts[0]
            for sh in (1, 2, 4, 8, 16):
                x = x | gather_lanes(x, lane ^ sh)
            value = lax.shift_right_logical(x, bit) & 1
            for o in range(owners):
                own = me_c == me_r * owners + o
                value = value | jnp.where(own, row_set[o * NI + a] & 1, 0)
            result.append(value)
        return result

    def exchange(axis, count, me, slot, send, recv):
        copies = []
        order = sorted(range(1, count), key=lambda s: -min(s, count - s))
        for step in order:
            copy = pltpu.make_async_remote_copy(
                src_ref=slot.at[0], dst_ref=slot.at[step],
                send_sem=send.at[step], recv_sem=recv.at[step],
                device_id={axis: lax.rem(me + step, count)}, device_id_type=MESH)
            copy.start()
            copies.append(copy)
        return copies

    def join_col(slot, copies):
        for copy in copies:
            copy.wait_recv()
        pairs = [any_of(slot[step, t] for step in range(C)) for t in range(NR // 2)]
        codes = pairs + [x >> 16 for x in pairs]
        return [(x << 31) >> 31 for x in codes], [(x << 30) >> 31 for x in codes]

    def turn():
        def step(k, carry):
            parts = [adj_ref[pl.ds(pl.multiple_of((NK * g + k) * wd, 8), wd), :] for g in range(G)]
            x = parts[0] if G == 1 else jnp.concatenate(parts, axis=0)
            turn_ref[...] = x.T
            for j in range(16):
                words_ref[k * 16 + j] = turn_ref[pl.ds(j, 8, stride=16), :]
            return carry

        repeat(NK, step, 0)

    def row_words(row_set):
        for h, mask in enumerate(row_set):
            x = (mask & 1) << (lane % 16)
            for sh in (1, 2, 4, 8):
                x = x | pltpu.roll(x, 128 - sh, 1)
            turn_ref[pl.ds(8 * h, 8), :] = x

    def tournament(row_set):
        kbits = log2(NK)
        row_words(row_set)

        def step(k, carry):
            f = zero
            for g in range(G):
                row = jnp.broadcast_to(turn_ref[pl.ds(NK * g + k, 1), :], (8, 128))
                f = jnp.where(lane // wd == g, gather_lanes(row, sub * 16), f)
            nodes = [[words_ref[k * 16 + j] & ((f << (31 - j)) >> 31)] for j in range(16)]
            while len(nodes) > 1:
                nodes = [merge(nodes[i], nodes[i + 1]) for i in range(0, len(nodes), 2)]
            node = nodes[0]
            rest = ~carry[0]
            fresh = node[0] & rest
            out = [carry[0] | node[0]]
            for p in range(4):
                out.append(carry[1 + p] | (node[1 + p] & rest))
            for p in range(kbits):
                out.append(carry[5 + p] | (fresh & -((k >> p) & 1)))
            return tuple(out)

        return list(repeat(NK, step, (zero,) * (5 + kbits)))

    for load in loads:
        load.wait()
    for t, tile in enumerate(pull([jnp.where(seeds(q)[0], 1, 0) for q in range(NI)])):
        col_buf[0, 0, t] = tile
    pl.semaphore_wait(barrier, R + C - 2)
    pend1 = exchange("col", C, me_c, col_buf.at[0], col_send.at[0], col_recv.at[0])
    turn()
    s1, s0 = join_col(col_buf.at[0], pend1)

    for t, tile in enumerate(push(s1)):
        row_buf[0, t] = tile
    pend2 = exchange("row", R, me_r, row_buf, row_send, row_recv)
    first_two = [tournament(s0), tournament(s1)]
    for copy in pend2:
        copy.wait_recv()
    col_set = [any_of(row_buf[step, t] for step in range(R)) for t in range(NI)]

    for t, tile in enumerate(pull(col_set)):
        col_buf[1, 0, t] = tile
    pend3 = exchange("col", C, me_c, col_buf.at[1], col_send.at[1], col_recv.at[1])
    s3, s2 = join_col(col_buf.at[1], pend3)

    nodes = first_two + [tournament(s2), tournament(s3)]
    have = [node[0] for node in nodes]
    planes = list(nodes[0][1:])
    for d in range(1, LEVELS):
        fresh = have[d] & ~have[d - 1]
        planes = [p | (q & fresh) for p, q in zip(planes, nodes[d][1:])]
    kbits = log2(NK)
    where = list(range(4)) + [7 + p for p in range(kbits)]

    def fold(have, planes, turned, by_step):
        have_hi = [turned(x) for x in have]
        planes_hi = [turned(x) for x in planes]
        better = any_of(b & ~a for a, b in zip(have, have_hi))
        if by_step:
            same = ~any_of(a ^ b for a, b in zip(have, have_hi))
            less = None
            for a, b in zip(planes[4:4 + kbits], planes_hi[4:4 + kbits]):
                now = a & ~b
                less = now if less is None else now | (less & ~(a ^ b))
            if less is not None:
                better = better | (same & less)
        keep = ~better
        planes = [(a & keep) | (b & better) for a, b in zip(planes, planes_hi)] + [better]
        return [a | b for a, b in zip(have, have_hi)], planes

    for i in range(3):
        have, planes = fold(have, planes, lambda x: pltpu.roll(x, 8 - (1 << i), 0), True)
        where.append(4 + i)
    for i in range(log2(G)):
        have, planes = fold(have, planes, lambda x: pltpu.roll(x, 128 - (wd << i), 1), False)
        where.append(7 + kbits + i)

    have = [jnp.broadcast_to(x[0:1, :], (8, 128)) for x in have]
    planes = [jnp.broadcast_to(x[0:1, :], (8, 128)) for x in planes]
    for q in range(NI):
        idx = (sub + 8 * q) * 4 + lane // 32

        def bits(x):
            return lax.shift_right_logical(gather_lanes(x, idx), bit) & 1

        key = jnp.full((8, 128), (LEVELS + 1) * total, jnp.int32)
        for x in have:
            key = key - bits(x) * total
        parent = jnp.full((8, 128), me_r * height, jnp.int32)
        for p, x in zip(where, planes):
            parent = parent + (bits(x) << p)
        key_buf[0, q] = key + parent
    pend4 = exchange("row", R, me_r, key_buf, key_send, key_recv)
    for copy in pend4:
        copy.wait_recv()
    for q in range(NI):
        key = key_buf[0, q]
        for step in range(1, R):
            key = jnp.minimum(key, key_buf[step, q])
        seed, vid = seeds(q)
        key_ref[pl.ds(8 * q, 8), :] = jnp.where(seed, vid, key)
    for copy in pend1 + pend2 + pend3 + pend4:
        copy.wait_send()


def solution(mesh):
    R, C = mesh.shape["row"], mesh.shape["col"]

    def local(adjacency, seed_mask, source):
        height, wd = adjacency.shape
        width = seed_mask.shape[0]
        total = R * height
        G = 128 // wd
        NI = width // 1024
        NR = height // 1024
        vmem = pl.BlockSpec(memory_space=pltpu.VMEM)
        DMA = pltpu.SemaphoreType.DMA
        key = pl.pallas_call(
            functools.partial(kernel, R, C),
            out_shape=jax.ShapeDtypeStruct((width // 128, 128), jnp.int32),
            in_specs=[pl.BlockSpec(memory_space=pl.ANY), vmem, pl.BlockSpec(memory_space=pltpu.SMEM)],
            out_specs=vmem,
            scratch_shapes=[
                pltpu.VMEM((height // 128 * wd, 128), jnp.int32),
                DMA((height // 128,)),
                pltpu.VMEM((128, 128), jnp.int32),
                pltpu.VMEM((height // 8 // G, 8, 128), jnp.int32),
                pltpu.VMEM((2, C, NR // 2, 8, 128), jnp.int32),
                pltpu.VMEM((R, NI, 8, 128), jnp.int32),
                pltpu.VMEM((R, NI, 8, 128), jnp.int32),
                DMA((2, C)), DMA((2, C)), DMA((R,)), DMA((R,)), DMA((R,)), DMA((R,)),
            ],
            compiler_params=pltpu.CompilerParams(collective_id=0, has_side_effects=True),
        )(adjacency.T, seed_mask.reshape(width // 128, 128), source)
        key = key.reshape(width)
        level = jnp.zeros_like(key)
        for d in range(1, LEVELS + 1):
            level = level + (key >= d * total).astype(jnp.int32)
        none = key >= (LEVELS + 1) * total
        return jnp.where(none, -1, level), jnp.where(none, -1, key - level * total)

    in_specs = (P("row", "col"), P("col"), P())
    out_specs = (P("col"), P("col"))
    return jax.shard_map(local, mesh=mesh, in_specs=in_specs, out_specs=out_specs, check_vma=False)
```

time: 28.6 us -> 25.1 us (0.88)
  local copies, waits for them, and re-layouts: 4.2 us -> 0 us
  other arithmetic: 0 us -> 1.28 us
  Pallas kernels: 22.9 us -> 22.3 us
    unnamed x7 -> x0, local copies, waits for them, and re-layouts: 4.2 us -> none
    select_n x0 -> x1, other arithmetic: none -> 1.28 us  [local(): jnp.where(none, -1, key - level * total)]
    pallas_call x1, Pallas kernels: 22.9 us -> 22.3 us  [local(): pl.pallas_call(functools.partial(kernel, R, C), out_shape=jax.ShapeDtypeS...]
where the time goes in v2:
time: 25.1 us; the launch traced here: 24.9 us
  Pallas kernels  22.3 us (89%)
  other arithmetic  1.28 us (5%)
  between operations  1.28 us (5%)
    pallas_call x1, Pallas kernels, local(): pl.pallas_call(functools.partial(kernel, R, C), out_shape=jax.ShapeDtypeS...  22.3 us
    select_n x1, other arithmetic, local(): jnp.where(none, -1, key - level * total)  1.28 us

profile of v2, /device:TPU:0, one launch (start us, length us, event | category | flops | bytes accessed | tf_op | source)
XLA Modules:
  0.0 24.9 jit_solution(1131280521959571034)
XLA Ops:
  1.3 22.3 %shard_map.50 = s32[8,128]{1,0:T(8,128)} custom-call(s32[32,2048]{1,0:T(8,128)} %bitcast.29, s32[8,128]{1,0:T(8,128)} %bitcast.30, s32[1]{0:T(128)S(6)} %copy.5.src_ref), custom_call_target="tpu_custom_call" | custom-call | tf_op jit(solution)/shard_map/pallas_call | solution.py:296
  23.6 1.3 %fusion = (s32[1024]{0:T(1024)}, s32[1024]{0:T(1024)}) fusion(s32[8,128]{1,0:T(8,128)} %shard_map.50), kind=kLoop, calls=%fused_computation.6 | loop fusion | flops 16384 | bytes 12288 | tf_op jit(solution)/shard_map/jit(_where)/select_n | solution.py:318

commit v3 on v2

--- a/solution.py
+++ b/solution.py
@@ -18,6 +18,10 @@
 
 def gather_lanes(x, idx):
     return jnp.take_along_axis(x, idx, axis=1)
+
+
+def far_first(count):
+    return sorted(range(1, count), key=lambda s: -min(s, count - s))
 
 
 def any_of(values):
@@ -45,15 +49,22 @@
     return out
 
 
-def kernel(R, C, hbm_ref, seed_ref, src_ref, key_ref,
-           adj_ref, load_sem, turn_ref, words_ref, col_buf, row_buf, key_buf,
+def kernel(R, C, hbm_ref, seed_hbm, src_ref, key_ref,
+           adj_ref, load_sem, seed_ref, small_sem, turn_ref, words_ref, col_buf, row_buf, key_buf,
            col_send, col_recv, row_send, row_recv, key_send, key_recv):
     me_r = lax.axis_index("row")
     me_c = lax.axis_index("col")
+    barrier = pltpu.get_barrier_semaphore()
+    for step in far_first(C):
+        pl.semaphore_signal(barrier, inc=1, device_id={"col": lax.rem(me_c + step, C)}, device_id_type=MESH)
+    for step in far_first(R):
+        pl.semaphore_signal(barrier, inc=1, device_id={"row": lax.rem(me_r + step, R)}, device_id_type=MESH)
+
     wd, height = hbm_ref.shape
+    small = pltpu.make_async_copy(seed_hbm, seed_ref, small_sem)
     loads = [pltpu.make_async_copy(hbm_ref.at[:, pl.ds(128 * t, 128)], adj_ref.at[pl.ds(wd * t, wd), :], load_sem.at[t])
              for t in range(height // 128)]
-    for load in loads:
+    for load in [small] + loads:
         load.start()
     G = 128 // wd
     NI = wd // 32
@@ -62,16 +73,11 @@
     owners = NR // NI
     total = R * height
 
-    barrier = pltpu.get_barrier_semaphore()
-    for step in range(1, C):
-        pl.semaphore_signal(barrier, inc=1, device_id={"col": lax.rem(me_c + step, C)}, device_id_type=MESH)
-    for step in range(1, R):
-        pl.semaphore_signal(barrier, inc=1, device_id={"row": lax.rem(me_r + step, R)}, device_id_type=MESH)
-
     lane = lax.broadcasted_iota(jnp.int32, (8, 128), 1)
     sub = lax.broadcasted_iota(jnp.int32, (8, 128), 0)
     bit = lane % 32
     zero = jnp.zeros((8, 128), jnp.int32)
+    small.wait()
     source = src_ref[0]
     first = me_c * (wd * 32)
 
@@ -140,8 +146,7 @@
 
     def exchange(axis, count, me, slot, send, recv):
         copies = []
-        order = sorted(range(1, count), key=lambda s: -min(s, count - s))
-        for step in order:
+        for step in far_first(count):
             copy = pltpu.make_async_remote_copy(
                 src_ref=slot.at[0], dst_ref=slot.at[step],
                 send_sem=send.at[step], recv_sem=recv.at[step],
@@ -295,12 +300,14 @@
         DMA = pltpu.SemaphoreType.DMA
         key = pl.pallas_call(
             functools.partial(kernel, R, C),
-            out_shape=jax.ShapeDtypeStruct((width // 128, 128), jnp.int32),
-            in_specs=[pl.BlockSpec(memory_space=pl.ANY), vmem, pl.BlockSpec(memory_space=pltpu.SMEM)],
+            out_shape=pltpu.VMEM((width // 128, 128), jnp.int32),
+            in_specs=[pl.BlockSpec(memory_space=pl.ANY)] * 2 + [pl.BlockSpec(memory_space=pltpu.SMEM)],
             out_specs=vmem,
             scratch_shapes=[
                 pltpu.VMEM((height // 128 * wd, 128), jnp.int32),
                 DMA((height // 128,)),
+                pltpu.VMEM((width // 128, 128), jnp.int32),
+                DMA(()),
                 pltpu.VMEM((128, 128), jnp.int32),
                 pltpu.VMEM((height // 8 // G, 8, 128), jnp.int32),
                 pltpu.VMEM((2, C, NR // 2, 8, 128), jnp.int32),

time: 25.1 us -> 23.2 us (0.924)
  Pallas kernels: 22.3 us -> 21.1 us
  other arithmetic: 1.28 us -> 0.6 us
    pallas_call x1, Pallas kernels: 22.3 us -> 21.1 us  [local(): pl.pallas_call(functools.partial(kernel, R, C), out_shape=pltpu.VMEM((wid...]
    select_n x1, other arithmetic: 1.28 us -> 0.6 us  [local(): jnp.where(none, -1, key - level * total)]
where the time goes in v3:
time: 23.2 us; the launch traced here: 23 us
  Pallas kernels  21.1 us (91%)
  between operations  1.28 us (6%)
  other arithmetic  0.6 us (3%)
    pallas_call x1, Pallas kernels, local(): pl.pallas_call(functools.partial(kernel, R, C), out_shape=pltpu.VMEM((wid...  21.1 us
    select_n x1, other arithmetic, local(): jnp.where(none, -1, key - level * total)  0.6 us

profile of v3, /device:TPU:0, one launch (start us, length us, event | category | flops | bytes accessed | tf_op | source)
XLA Modules:
  0.0 23.0 jit_solution(7219045624726735840)
XLA Ops:
  1.3 21.1 %shard_map.50 = s32[8,128]{1,0:T(8,128)S(1)} custom-call(s32[32,2048]{1,0:T(8,128)} %bitcast.29, s32[8,128]{1,0:T(8,128)} %bitcast.30, s32[1]{0:T(128)S(6)} %copy.5.src_ref), custom_call_target="tpu_custom_call" | custom-call | tf_op jit(solution)/shard_map/pallas_call | solution.py:301
  22.4 0.6 %fusion = (s32[1024]{0:T(1024)}, s32[1024]{0:T(1024)}) fusion(s32[8,128]{1,0:T(8,128)S(1)} %shard_map.50), kind=kLoop, calls=%fused_computation.6 | loop fusion | flops 16384 | bytes 12288 | tf_op jit(solution)/shard_map/jit(_where)/select_n | solution.py:325

commit v4 on v3

--- a/solution.py
+++ b/solution.py
@@ -173,36 +173,41 @@
 
         repeat(NK, step, 0)
 
-    def row_words(row_set):
-        for h, mask in enumerate(row_set):
-            x = (mask & 1) << (lane % 16)
+    def row_words(nxt, now):
+        at = lane % 16
+        for h in range(NR):
+            x = ((nxt[h] & 1) << at) | ((now[h] & 1) << (at + 16))
             for sh in (1, 2, 4, 8):
                 x = x | pltpu.roll(x, 128 - sh, 1)
             turn_ref[pl.ds(8 * h, 8), :] = x
 
-    def tournament(row_set):
+    def tournaments(nxt, now):
         kbits = log2(NK)
-        row_words(row_set)
-
-        def step(k, carry):
+        row_words(nxt, now)
+
+        def step(k, carries):
             f = zero
             for g in range(G):
                 row = jnp.broadcast_to(turn_ref[pl.ds(NK * g + k, 1), :], (8, 128))
                 f = jnp.where(lane // wd == g, gather_lanes(row, sub * 16), f)
-            nodes = [[words_ref[k * 16 + j] & ((f << (31 - j)) >> 31)] for j in range(16)]
-            while len(nodes) > 1:
-                nodes = [merge(nodes[i], nodes[i + 1]) for i in range(0, len(nodes), 2)]
-            node = nodes[0]
-            rest = ~carry[0]
-            fresh = node[0] & rest
-            out = [carry[0] | node[0]]
-            for p in range(4):
-                out.append(carry[1 + p] | (node[1 + p] & rest))
-            for p in range(kbits):
-                out.append(carry[5 + p] | (fresh & -((k >> p) & 1)))
-            return tuple(out)
-
-        return list(repeat(NK, step, (zero,) * (5 + kbits)))
+            leaves = [words_ref[k * 16 + j] for j in range(16)]
+            outs = []
+            for top, carry in zip((15, 31), carries):
+                nodes = [[leaves[j] & ((f << (top - j)) >> 31)] for j in range(16)]
+                while len(nodes) > 1:
+                    nodes = [merge(nodes[i], nodes[i + 1]) for i in range(0, len(nodes), 2)]
+                node = nodes[0]
+                rest = ~carry[0]
+                fresh = node[0] & rest
+                out = [carry[0] | node[0]]
+                for p in range(4):
+                    out.append(carry[1 + p] | (node[1 + p] & rest))
+                for p in range(kbits):
+                    out.append(carry[5 + p] | (fresh & -((k >> p) & 1)))
+                outs.append(tuple(out))
+            return tuple(outs)
+
+        return list(repeat(NK, step, ((zero,) * (5 + kbits),) * 2))
 
     for load in loads:
         load.wait()
@@ -216,7 +221,7 @@
     for t, tile in enumerate(push(s1)):
         row_buf[0, t] = tile
     pend2 = exchange("row", R, me_r, row_buf, row_send, row_recv)
-    first_two = [tournament(s0), tournament(s1)]
+    first_two = tournaments(s1, s0)
     for copy in pend2:
         copy.wait_recv()
     col_set = [any_of(row_buf[step, t] for step in range(R)) for t in range(NI)]
@@ -226,7 +231,7 @@
     pend3 = exchange("col", C, me_c, col_buf.at[1], col_send.at[1], col_recv.at[1])
     s3, s2 = join_col(col_buf.at[1], pend3)
 
-    nodes = first_two + [tournament(s2), tournament(s3)]
+    nodes = first_two + tournaments(s3, s2)
     have = [node[0] for node in nodes]
     planes = list(nodes[0][1:])
     for d in range(1, LEVELS):

time: 23.2 us -> 23.1 us (level)
  no operation moved by 1% of the time
where the time goes in v4:
time: 23.1 us; the launch traced here: 23 us
  Pallas kernels  21.1 us (91%)
  between operations  1.28 us (6%)
  other arithmetic  0.6 us (3%)
    pallas_call x1, Pallas kernels, local(): pl.pallas_call(functools.partial(kernel, R, C), out_shape=pltpu.VMEM((wid...  21.1 us
    select_n x1, other arithmetic, local(): jnp.where(none, -1, key - level * total)  0.6 us

profile of v4, /device:TPU:0, one launch (start us, length us, event | category | flops | bytes accessed | tf_op | source)
XLA Modules:
  0.0 23.0 jit_solution(6262207526708499628)
XLA Ops:
  1.3 21.1 %shard_map.50 = s32[8,128]{1,0:T(8,128)S(1)} custom-call(s32[32,2048]{1,0:T(8,128)} %bitcast.29, s32[8,128]{1,0:T(8,128)} %bitcast.30, s32[1]{0:T(128)S(6)} %copy.5.src_ref), custom_call_target="tpu_custom_call" | custom-call | tf_op jit(solution)/shard_map/pallas_call | solution.py:306
  22.3 0.6 %fusion = (s32[1024]{0:T(1024)}, s32[1024]{0:T(1024)}) fusion(s32[8,128]{1,0:T(8,128)S(1)} %shard_map.50), kind=kLoop, calls=%fused_computation.6 | loop fusion | flops 16384 | bytes 12288 | tf_op jit(solution)/shard_map/jit(_where)/select_n | solution.py:330

commit v5 on v4

--- a/solution.py
+++ b/solution.py
@@ -279,6 +279,8 @@
             parent = parent + (bits(x) << p)
         key_buf[0, q] = key + parent
     pend4 = exchange("row", R, me_r, key_buf, key_send, key_recv)
+    for copy in pend1 + pend2 + pend3:
+        copy.wait_send()
     for copy in pend4:
         copy.wait_recv()
     for q in range(NI):
@@ -287,7 +289,7 @@
             key = jnp.minimum(key, key_buf[step, q])
         seed, vid = seeds(q)
         key_ref[pl.ds(8 * q, 8), :] = jnp.where(seed, vid, key)
-    for copy in pend1 + pend2 + pend3 + pend4:
+    for copy in pend4:
         copy.wait_send()
 
 

time: 23.1 us -> 23.1 us (level)
  no operation moved by 1% of the time
where the time goes in v5:
time: 23.1 us; the launch traced here: 22.9 us
  Pallas kernels  21 us (91%)
  between operations  1.28 us (6%)
  other arithmetic  0.6 us (3%)
    pallas_call x1, Pallas kernels, local(): pl.pallas_call(functools.partial(kernel, R, C), out_shape=pltpu.VMEM((wid...  21 us
    select_n x1, other arithmetic, local(): jnp.where(none, -1, key - level * total)  0.6 us

profile of v5, /device:TPU:0, one launch (start us, length us, event | category | flops | bytes accessed | tf_op | source)
XLA Modules:
  0.0 22.9 jit_solution(5957134687577506131)
XLA Ops:
  1.3 21.0 %shard_map.50 = s32[8,128]{1,0:T(8,128)S(1)} custom-call(s32[32,2048]{1,0:T(8,128)} %bitcast.29, s32[8,128]{1,0:T(8,128)} %bitcast.30, s32[1]{0:T(128)S(6)} %copy.5.src_ref), custom_call_target="tpu_custom_call" | custom-call | tf_op jit(solution)/shard_map/pallas_call | solution.py:308
  22.3 0.6 %fusion = (s32[1024]{0:T(1024)}, s32[1024]{0:T(1024)}) fusion(s32[8,128]{1,0:T(8,128)S(1)} %shard_map.50), kind=kLoop, calls=%fused_computation.6 | loop fusion | flops 16384 | bytes 12288 | tf_op jit(solution)/shard_map/jit(_where)/select_n | solution.py:332
